TPU v7x, 32 devices: a whole 2x2x4 slice. The times are simulated.
32 devices in a mesh: gx: 4 (over x, core), gy: 4 (over z), gz: 2 (over y).
Axes of the slice: x: 2, y: 2, z: 4, core: 2. Of those that a mesh axis runs over, the one named last changes fastest.
Arguments:
- particle_fields: float32 [20, 262144], P(None, ('gx', 'gy', 'gz')), may hold values from -4 to 4
- step_length: float32 [262144], P(('gx', 'gy', 'gz')), may hold values from 0.1 to 1
- live_mask: int32 [262144], P(('gx', 'gy', 'gz')), may hold values 0 or 1
- dest_cell: int32 [262144], P(('gx', 'gy', 'gz')), may hold values from 0 to 511
- block_counts: int32 [32, 6], P(('gx', 'gy', 'gz')), may hold values from 0 to 12, as said below
- block_lists: int32 [32, 48], P(('gx', 'gy', 'gz')), may hold values from 0 to 87, as said below
Outputs:
- tile_sums: float32 [20, 16384], P(None, ('gx', 'gy', 'gz'))
Inputs may be any that keep to these rules, and one draw needn't show every extreme that they name: `block_counts`: columns are directions in the order x lower, x upper, z lower, z upper, y lower, y upper; a count is at most its section's span (6, 6 or 12) and may be 0; at every section some domain receives full spans from both neighbours. `block_lists`: per domain, 6 entries toward the lower x neighbour, 6 toward the upper, then 2 * 6 for z and 24 for y in the same way; entries are block numbers of the domain's pool at that section. Entries below their direction's count are valid: valid entries of one domain over all sections are distinct, and each names an own block or an appended block that its sender filled. Other entries are arbitrary numbers within the pool.
All inputs are finite; a program needn't handle non-finite values. No bound on the sum of `live_mask` on one device may be relied on, other than what follows from the above.
Results may differ from a plain program's by a relative error of at most 0.0003.
Values sent between devices are 32-bit elements; how exact they have to be, the bound alone decides.
A program may use at most 64 MiB of HBM per device.

v0:
```python
import functools

import jax
import jax.numpy as jnp
from jax import lax
from jax.experimental import pallas as pl
from jax.experimental.pallas import tpu as pltpu
from jax.sharding import PartitionSpec as P

CELLS = 512
CAP_X = 6
CAP_Z = 6
CAP_Y = 12
LANES = 128
HALF = 256
GROUP = 8
GONE = 8 * CELLS
CLASSES = 3


def migrate_kernel(
    sizes,
    counts,
    lists,
    lists_row,
    fields_hbm,
    step_hbm,
    live_hbm,
    cell_hbm,
    out_ref,
    fields,
    step,
    live,
    cell,
    pool,
    offsets,
    acc,
    sent_x,
    sent_z,
    got_x,
    got_z,
    sent_y,
    got_y,
    load_sem,
    send_sem,
    recv_sem,
):
    field_count = fields_hbm.shape[0]
    rows = pool.shape[1]
    whole = field_count // 8 * 8
    tail = field_count - whole
    blocks = step.shape[0]

    me = {axis: lax.axis_index(axis) for axis in ("gx", "gy", "gz")}
    lower = {axis: {axis: lax.rem(me[axis] + sizes[axis] - 1, sizes[axis])} for axis in me}
    upper = {axis: {axis: lax.rem(me[axis] + 1, sizes[axis])} for axis in me}

    loads = [
        pltpu.make_async_copy(fields_hbm, fields, load_sem.at[0]),
        pltpu.make_async_copy(step_hbm, step, load_sem.at[1]),
        pltpu.make_async_copy(live_hbm, live, load_sem.at[2]),
        pltpu.make_async_copy(cell_hbm, cell, load_sem.at[3]),
    ]
    for load in loads:
        load.start()

    barrier = pltpu.get_barrier_semaphore()
    for axis in me:
        for neighbour in (lower[axis], upper[axis]):
            pl.semaphore_signal(
                barrier, inc=1, device_id=neighbour, device_id_type=pl.DeviceIdType.MESH
            )

    spans = (CAP_X, CAP_X, CAP_Z, CAP_Z, CAP_Y, CAP_Y)
    lane = lax.broadcasted_iota(jnp.int32, lists_row.shape, 1)
    limit = jnp.zeros(lists_row.shape, jnp.int32)
    away = jnp.zeros(lists_row.shape, jnp.float32)
    start = 0
    for k, span in enumerate(spans):
        here = lane >= start
        limit = jnp.where(here, counts[0, k] + start, limit)
        away = jnp.where(here, float(GONE if k < 4 else (k - 3) * CELLS), away)
        start += span
    away = jnp.where(lane < limit, away, 0.0)
    number = lax.broadcasted_iota(jnp.int32, (offsets.shape[0], lists_row.shape[1]), 0)
    named = jnp.where(lists_row[...] == number, away, 0.0)
    offsets[...] = jnp.broadcast_to(jnp.sum(named, axis=1, keepdims=True), offsets.shape)

    for load in loads:
        load.wait()

    first_row = lax.broadcasted_iota(jnp.int32, (8, LANES), 0)

    def own_block(e):
        v = fields[:, pl.ds(pl.multiple_of(e * LANES, LANES), LANES)]
        top = v[:8]
        pace = step[pl.ds(e, 1), :]
        top = top + jnp.where(first_row < 3, pace * pltpu.roll(top, 5, 0), 0.0)
        v = jnp.concatenate([top, v[8:]], axis=0)
        v = v * live[pl.ds(e, 1), :].astype(jnp.float32)
        where_to = cell[pl.ds(e, 1), :].astype(jnp.float32)
        return jnp.concatenate(
            [v, jnp.broadcast_to(where_to, (rows - field_count, LANES))], axis=0
        )

    def exchange(axis, index, sent, got, width):
        out = []
        for side, (target, other) in enumerate(((lower, 1), (upper, 0))):
            copy = pltpu.make_async_remote_copy(
                src_ref=sent.at[pl.ds(side * width, width)],
                dst_ref=got.at[pl.ds(other * width, width)],
                send_sem=send_sem.at[index + side],
                recv_sem=recv_sem.at[index + other],
                device_id=target[axis],
                device_id_type=pl.DeviceIdType.MESH,
            )
            copy.start()
            out.append(copy)
        return out

    def fill(sent, slot, span, first_entry, first_count):
        count = jnp.full((rows, LANES), counts[0, first_count + slot // span])
        block = pool[lists[0, first_entry + slot]]
        block = jnp.where(count > slot % span, block, 0.0)
        side, i = slot // span, slot % span
        sent[side, pl.ds(i * whole, whole), :] = block[:whole]
        tail_at = span * whole + i * tail
        sent[side, pl.ds(tail_at, tail), :] = block[whole:field_count]
        sent[side, pl.ds(span * field_count + i, 1), :] = block[field_count : field_count + 1]

    def unpacked(got, slot, span):
        side, i = slot // span, slot % span
        body = got[side, pl.ds(i * whole, whole), :]
        rest = got[side, pl.ds(span * whole + i * tail, tail), :]
        cells = got[side, pl.ds(span * field_count + i, 1), :]
        spare = jnp.broadcast_to(cells, (rows - field_count, LANES))
        return jnp.concatenate([body, rest, spare], axis=0), cells

    def advance(g, carry):
        for i in range(GROUP):
            pool[g * GROUP + i] = own_block(g * GROUP + i)
        return carry

    lax.fori_loop(0, blocks // GROUP, advance, 0)
    for slot in range(2 * CAP_X):
        fill(sent_x, slot, CAP_X, 0, 0)
    pl.semaphore_wait(barrier, 6)
    copies_x = exchange("gx", 0, sent_x, got_x, 1)

    code = lax.broadcasted_iota(jnp.int32, (HALF, LANES), 0).astype(jnp.float32)
    parts = CLASSES * CELLS // HALF

    def operands(v, cells, wanted=tuple(range(parts))):
        high = v.astype(jnp.bfloat16).astype(jnp.float32)
        both = jnp.concatenate([high, v - high], axis=0)
        part = jnp.floor(cells * (1.0 / HALF))
        inner = cells - part * HALF
        left = jnp.concatenate(
            [jnp.where(part == float(h), both, 0.0).astype(jnp.bfloat16) for h in wanted],
            axis=0,
        )
        right = jnp.where(code == inner, 1.0, 0.0).astype(jnp.bfloat16)
        return left, right

    def bin_group(pairs):
        left = jnp.concatenate([a for a, _ in pairs], axis=1)
        right = jnp.concatenate([b for _, b in pairs], axis=1)
        acc[...] += lax.dot_general(
            left, right, (((1,), (1,)), ((), ())), preferred_element_type=jnp.float32
        )

    acc[...] = jnp.zeros_like(acc)

    def bin_own(g, carry):
        pairs = []
        for i in range(GROUP):
            b = g * GROUP + i
            cells = pool[b, pl.ds(field_count, 1), :] + offsets[pl.ds(b, 1), :]
            pairs.append(operands(pool[b], cells))
        bin_group(pairs)
        return carry

    early = 3 * (blocks // GROUP) // 8
    lax.fori_loop(0, early, bin_own, 0)

    def bin_got(got, side, width, base, wanted=tuple(range(parts))):
        pairs = []
        for i in range(side * width, (side + 1) * width):
            v, cells = unpacked(got, i, width)
            pairs.append(operands(v, cells + offsets[pl.ds(base + i, 1), :], wanted))
        left = jnp.concatenate([a for a, _ in pairs], axis=1)
        right = jnp.concatenate([b for _, b in pairs], axis=1)
        acc[pl.ds(2 * rows * wanted[0], 2 * rows * len(wanted)), :] += lax.dot_general(
            left, right, (((1,), (1,)), ((), ())), preferred_element_type=jnp.float32
        )

    for copy in copies_x:
        copy.wait_recv()
    for slot in range(2 * CAP_X):
        pool[blocks + slot] = unpacked(got_x, slot, CAP_X)[0]
    for slot in range(2 * CAP_Z):
        fill(sent_z, slot, CAP_Z, 2 * CAP_X, 2)
    copies_z = exchange("gz", 2, sent_z, got_z, 1)
    lax.fori_loop(early, blocks // GROUP, bin_own, 0)
    bin_got(got_x, 0, CAP_X, blocks)
    bin_got(got_x, 1, CAP_X, blocks)

    kept_parts = tuple(range(CELLS // HALF))
    bound_parts = tuple(range(CELLS // HALF, parts))
    late = blocks + 2 * CAP_X
    for side in (1, 0):
        pltpu.make_async_remote_copy(
            src_ref=sent_z.at[pl.ds(1 - side, 1)],
            dst_ref=got_z.at[pl.ds(side, 1)],
            send_sem=send_sem.at[3 - side],
            recv_sem=recv_sem.at[2 + side],
            device_id=upper["gz"] if side == 0 else lower["gz"],
            device_id_type=pl.DeviceIdType.MESH,
        ).wait_recv()
        if side == 1:
            bin_got(got_z, side, CAP_Z, late)
        else:
            bin_got(got_z, side, CAP_Z, late, bound_parts)

    def bin_kept(base):
        bin_got(got_z, 0, CAP_Z, base, kept_parts)

    def halves(kind):
        tops = [2 * rows * h for h in range(kind * CELLS // HALF, (kind + 1) * CELLS // HALF)]
        return [
            (acc[pl.ds(t, rows), :] + acc[pl.ds(t + rows, rows), :])[:field_count] for t in tops
        ]

    for side in (0, 1):
        for i, half in enumerate(halves(side + 1)):
            sent_y[side, pl.ds(i * field_count, field_count), :] = half
    copies_y = exchange("gy", 4, sent_y, got_y, 1)
    bin_kept(late)
    kept = halves(0)
    for copy in copies_y:
        copy.wait_recv()
    for i, half in enumerate(kept):
        part = pl.ds(i * field_count, field_count)
        out_ref[:, pl.ds(i * HALF, HALF)] = half + got_y[0, part, :] + got_y[1, part, :]
    for copy in copies_x + copies_z + copies_y:
        copy.wait_send()


def solution(mesh):
    sizes = {axis: mesh.shape[axis] for axis in ("gx", "gy", "gz")}

    def per_device(particle_fields, step_length, live_mask, dest_cell, block_counts, block_lists):
        field_count, particles = particle_fields.shape
        blocks = particles // LANES
        rows = (field_count + 1 + 7) // 8 * 8
        sum_rows = (field_count * CELLS // HALF + 7) // 8 * 8
        pool_blocks = blocks + 2 * CAP_X + 2 * CAP_Z

        def packed(span):
            return (span * (field_count + 1) + 7) // 8 * 8

        by_block = [a.reshape(blocks, LANES) for a in (step_length, live_mask, dest_cell)]
        any_space = pl.BlockSpec(memory_space=pl.ANY)
        vmem = pl.BlockSpec(memory_space=pltpu.VMEM)
        smem = pl.BlockSpec(memory_space=pltpu.SMEM)
        f32 = jnp.float32
        return pl.pallas_call(
            functools.partial(migrate_kernel, sizes),
            out_shape=jax.ShapeDtypeStruct((field_count, CELLS), f32),
            in_specs=[smem, smem, vmem, any_space, any_space, any_space, any_space],
            out_specs=vmem,
            scratch_shapes=[
                pltpu.VMEM((field_count, particles), f32),
                pltpu.VMEM((blocks, LANES), f32),
                pltpu.VMEM((blocks, LANES), jnp.int32),
                pltpu.VMEM((blocks, LANES), jnp.int32),
                pltpu.VMEM((blocks + 2 * CAP_X, rows, LANES), f32),
                pltpu.VMEM((pool_blocks, LANES), f32),
                pltpu.VMEM((2 * rows * CLASSES * CELLS // HALF, HALF), f32),
                pltpu.VMEM((2, packed(CAP_X), LANES), f32),
                pltpu.VMEM((2, packed(CAP_Z), LANES), f32),
                pltpu.VMEM((2, packed(CAP_X), LANES), f32),
                pltpu.VMEM((2, packed(CAP_Z), LANES), f32),
                pltpu.VMEM((2, sum_rows, HALF), f32),
                pltpu.VMEM((2, sum_rows, HALF), f32),
                pltpu.SemaphoreType.DMA((4,)),
                pltpu.SemaphoreType.DMA((6,)),
                pltpu.SemaphoreType.DMA((6,)),
            ],
            compiler_params=pltpu.CompilerParams(collective_id=0, has_side_effects=True),
        )(block_counts, block_lists, block_lists, particle_fields, *by_block)

    placed = (
        P(None, ("gx", "gy", "gz")),
        P(("gx", "gy", "gz")),
        P(("gx", "gy", "gz")),
        P(("gx", "gy", "gz")),
        P(("gx", "gy", "gz"), None),
        P(("gx", "gy", "gz"), None),
    )
    return jax.shard_map(
        per_device,
        mesh=mesh,
        in_specs=placed,
        out_specs=P(None, ("gx", "gy", "gz")),
        check_vma=False,
    )
```

profile of v0, /device:TPU:0, one launch (start us, length us, event | category | flops | bytes accessed | tf_op | source)
XLA Modules:
  0.0 21.1 jit_solution(18296378650798866207)
XLA Ops:
  0.0 19.7 %shard_map.64 = f32[20,512]{1,0:T(8,128)} custom-call(s32[1,6]{1,0:T(1,128)} %counts.1, s32[1,48]{1,0:T(1,128)} %lists_row.1, s32[1,48]{1,0:T(1,128)} %lists_row.1, f32[20,8192]{1,0:T(8,128)} %fields_hbm.1, f32[64,128]{1,0:T(8,128)} %bitcast.3, s32[64,128]{1,0:T(8,128)} %bitcast.4, s32[64,128]{1,0:T(8,128)} %bitcast.5), custom_call_target="tpu_custom_call" | custom-call | tf_op jit(solution)/shard_map/pallas_call | solution.py:267
  19.7 1.4 %copy.8 = f32[20,512]{1,0:T(8,128)} copy(f32[20,512]{1,0:T(8,128)} %shard_map.64) | data formatting | bytes 81920
where the time goes:
time: 21.3 us; the launch traced here: 21.1 us
  Pallas kernels  19.7 us (92%)
  local copies, waits for them, and re-layouts  1.42 us (7%)
    pallas_call x1, Pallas kernels, per_device(): pl.pallas_call(functools.partial(migrate_kernel, sizes), out_shape=jax.Sh...  19.7 us
    unnamed x1, local copies, waits for them, and re-layouts  1.42 us

commit v1 on v0

--- a/solution.py
+++ b/solution.py
@@ -20,9 +20,8 @@
 
 def migrate_kernel(
     sizes,
-    counts,
-    lists,
-    lists_row,
+    counts_hbm,
+    lists_hbm,
     fields_hbm,
     step_hbm,
     live_hbm,
@@ -41,6 +40,9 @@
     got_z,
     sent_y,
     got_y,
+    counts,
+    lists,
+    lists_row,
     load_sem,
     send_sem,
     recv_sem,
@@ -55,13 +57,18 @@
     lower = {axis: {axis: lax.rem(me[axis] + sizes[axis] - 1, sizes[axis])} for axis in me}
     upper = {axis: {axis: lax.rem(me[axis] + 1, sizes[axis])} for axis in me}
 
+    small = [
+        pltpu.make_async_copy(counts_hbm, counts, load_sem.at[4]),
+        pltpu.make_async_copy(lists_hbm, lists, load_sem.at[5]),
+        pltpu.make_async_copy(lists_hbm, lists_row, load_sem.at[6]),
+    ]
     loads = [
         pltpu.make_async_copy(fields_hbm, fields, load_sem.at[0]),
         pltpu.make_async_copy(step_hbm, step, load_sem.at[1]),
         pltpu.make_async_copy(live_hbm, live, load_sem.at[2]),
         pltpu.make_async_copy(cell_hbm, cell, load_sem.at[3]),
     ]
-    for load in loads:
+    for load in loads + small:
         load.start()
 
     barrier = pltpu.get_barrier_semaphore()
@@ -71,6 +78,8 @@
                 barrier, inc=1, device_id=neighbour, device_id_type=pl.DeviceIdType.MESH
             )
 
+    for load in small:
+        load.wait()
     spans = (CAP_X, CAP_X, CAP_Z, CAP_Z, CAP_Y, CAP_Y)
     lane = lax.broadcasted_iota(jnp.int32, lists_row.shape, 1)
     limit = jnp.zeros(lists_row.shape, jnp.int32)
@@ -266,8 +275,8 @@
         f32 = jnp.float32
         return pl.pallas_call(
             functools.partial(migrate_kernel, sizes),
-            out_shape=jax.ShapeDtypeStruct((field_count, CELLS), f32),
-            in_specs=[smem, smem, vmem, any_space, any_space, any_space, any_space],
+            out_shape=pltpu.VMEM((field_count, CELLS), f32),
+            in_specs=[any_space] * 6,
             out_specs=vmem,
             scratch_shapes=[
                 pltpu.VMEM((field_count, particles), f32),
@@ -283,12 +292,15 @@
                 pltpu.VMEM((2, packed(CAP_Z), LANES), f32),
                 pltpu.VMEM((2, sum_rows, HALF), f32),
                 pltpu.VMEM((2, sum_rows, HALF), f32),
-                pltpu.SemaphoreType.DMA((4,)),
+                pltpu.SMEM(block_counts.shape, jnp.int32),
+                pltpu.SMEM(block_lists.shape, jnp.int32),
+                pltpu.VMEM(block_lists.shape, jnp.int32),
+                pltpu.SemaphoreType.DMA((7,)),
                 pltpu.SemaphoreType.DMA((6,)),
                 pltpu.SemaphoreType.DMA((6,)),
             ],
             compiler_params=pltpu.CompilerParams(collective_id=0, has_side_effects=True),
-        )(block_counts, block_lists, block_lists, particle_fields, *by_block)
+        )(block_counts, block_lists, particle_fields, *by_block)
 
     placed = (
         P(None, ("gx", "gy", "gz")),

time: 21.3 us -> 19.2 us (0.901)
  Pallas kernels: 19.7 us -> 18.4 us
  local copies, waits for them, and re-layouts: 1.42 us -> 0.62 us
    pallas_call x1, Pallas kernels: 19.7 us -> 18.4 us  [per_device(): pl.pallas_call(functools.partial(migrate_kernel, sizes), out_shape=pltpu....]
    unnamed x1, local copies, waits for them, and re-layouts: 1.42 us -> 0.62 us
where the time goes in v1:
time: 19.2 us; the launch traced here: 19 us
  Pallas kernels  18.4 us (96%)
  local copies, waits for them, and re-layouts  0.62 us (3%)
    pallas_call x1, Pallas kernels, per_device(): pl.pallas_call(functools.partial(migrate_kernel, sizes), out_shape=pltpu....  18.4 us
    unnamed x1, local copies, waits for them, and re-layouts  0.62 us

profile of v1, /device:TPU:0, one launch (start us, length us, event | category | flops | bytes accessed | tf_op | source)
XLA Modules:
  0.0 19.0 jit_solution(11741967194181973429)
XLA Ops:
  0.0 18.4 %shard_map.64 = f32[20,512]{1,0:T(8,128)S(1)} custom-call(s32[1,6]{1,0:T(1,128)} %counts_hbm.1, s32[1,48]{1,0:T(1,128)} %lists_hbm.1, f32[20,8192]{1,0:T(8,128)} %fields_hbm.1, f32[64,128]{1,0:T(8,128)} %bitcast.3, s32[64,128]{1,0:T(8,128)} %bitcast.4, s32[64,128]{1,0:T(8,128)} %bitcast.5), custom_call_target="tpu_custom_call" | custom-call | tf_op jit(solution)/shard_map/pallas_call | solution.py:276
  18.4 0.6 %copy.8 = f32[20,512]{1,0:T(8,128)} copy(f32[20,512]{1,0:T(8,128)S(1)} %shard_map.64) | data formatting | bytes 81920

commit v2 on v1

v2 whole, which is shorter than its diff:
```python
import functools

import jax
import jax.numpy as jnp
from jax import lax
from jax.experimental import pallas as pl
from jax.experimental.pallas import tpu as pltpu
from jax.sharding import PartitionSpec as P

CELLS = 512
CAP_X = 6
CAP_Z = 6
CAP_Y = 12
LANES = 128
HALF = 256
GROUP = 8
GONE = 16 * CELLS
AXES = ("gx", "gy", "gz")


def plan(sizes):
    steps_z = (1,) if sizes["gz"] == 2 else (-1, 1)
    classes = [{}, {"gy": -1}, {"gy": 1}]
    for dz in steps_z:
        classes += [{"gz": dz}, {"gz": dz, "gy": -1}, {"gz": dz, "gy": 1}]
    return steps_z, classes


def migrate_kernel(
    sizes,
    counts_hbm,
    lists_hbm,
    fields_hbm,
    step_hbm,
    live_hbm,
    cell_hbm,
    out_ref,
    fields,
    step,
    live,
    cell,
    offsets,
    offsets_x,
    offsets_slot,
    acc_kept,
    acc,
    sent_x,
    got_x,
    sent_meta,
    got_meta,
    sent,
    got,
    counts,
    lists,
    lists_row,
    load_sem,
    send_x_sem,
    recv_x_sem,
    send_meta_sem,
    recv_meta_sem,
    send_sem,
    recv_sem,
):
    steps_z, classes = plan(sizes)
    field_count = fields_hbm.shape[0]
    rows = (field_count + 1 + 7) // 8 * 8
    whole = field_count // 8 * 8
    tail = field_count - whole
    blocks = step.shape[0]
    halves = CELLS // HALF
    start_z, start_y = 2 * CAP_X, 2 * CAP_X + 2 * CAP_Z

    me = {axis: lax.axis_index(axis) for axis in AXES}

    def target(moves):
        return {a: lax.rem(me[a] + sizes[a] + d, sizes[a]) for a, d in moves.items()}

    def remote(src, dst, send, recv, moves):
        return pltpu.make_async_remote_copy(
            src_ref=src,
            dst_ref=dst,
            send_sem=send,
            recv_sem=recv,
            device_id=target(moves),
            device_id_type=pl.DeviceIdType.MESH,
        )

    loads = [
        pltpu.make_async_copy(src, dst, load_sem.at[i])
        for i, (src, dst) in enumerate(
            [
                (counts_hbm, counts),
                (lists_hbm, lists),
                (lists_hbm, lists_row),
                (step_hbm, step),
                (live_hbm, live),
                (cell_hbm, cell),
                (fields_hbm, fields),
            ]
        )
    ]
    for load in loads:
        load.start()

    moves_x = ({"gx": -1}, {"gx": 1})
    partners = {}
    for moves in list(moves_x) + classes[1:]:
        partners[tuple(moves.get(a, 0) % sizes[a] for a in AXES)] = moves
    barrier = pltpu.get_barrier_semaphore()
    for moves in partners.values():
        pl.semaphore_signal(
            barrier, inc=1, device_id=target(moves), device_id_type=pl.DeviceIdType.MESH
        )

    for load in loads:
        load.wait()

    first_row = lax.broadcasted_iota(jnp.int32, (8, LANES), 0)

    def own_block(e):
        v = fields[:, pl.ds(e * LANES, LANES)]
        top = v[:8]
        pace = step[pl.ds(e, 1), :]
        top = top + jnp.where(first_row < 3, pace * pltpu.roll(top, 5, 0), 0.0)
        v = jnp.concatenate([top, v[8:]], axis=0)
        v = v * live[pl.ds(e, 1), :].astype(jnp.float32)
        where_to = cell[pl.ds(e, 1), :].astype(jnp.float32)
        spare = jnp.broadcast_to(where_to, (rows - field_count, LANES))
        return jnp.concatenate([v, spare], axis=0), where_to

    for slot in range(2 * CAP_X):
        block, _ = own_block(jnp.minimum(lists[0, slot], blocks - 1))
        side, i = slot // CAP_X, slot % CAP_X
        count = jnp.full((rows, LANES), counts[0, side])
        block = jnp.where(count > i, block, 0.0)
        sent_x[side, pl.ds(i * whole, whole), :] = block[:whole]
        sent_x[side, pl.ds(CAP_X * whole + i * tail, tail), :] = block[whole:field_count]
        sent_x[side, pl.ds(CAP_X * field_count + i, 1), :] = block[field_count : field_count + 1]

    pl.semaphore_wait(barrier, len(partners))

    def copy_x(side):
        return [
            remote(
                sent_x.at[pl.ds(s, 1)],
                got_x.at[pl.ds(s, 1)],
                send_x_sem.at[s],
                recv_x_sem.at[s],
                moves_x[s],
            )
            for s in side
        ]

    copies_x = copy_x((0, 1))
    for copy in copies_x:
        copy.start()

    lane = lax.broadcasted_iota(jnp.int32, lists_row.shape, 1)
    z_number = blocks + 2 * CAP_X + jnp.where(
        lane < start_z + CAP_Z, lane - start_z + CAP_Z, lane - start_z - CAP_Z
    )
    onward = jnp.zeros(lists_row.shape, jnp.float32)
    for k in range(2 * CAP_Y):
        side, i = k // CAP_Y, k % CAP_Y
        count = jnp.full(lists_row.shape, counts[0, 4 + side])
        hit = (z_number == lists[0, start_y + k]) & (count > i)
        onward = jnp.where(hit, float(1 + side), onward)
    sent_meta[...] = jnp.broadcast_to(onward, sent_meta.shape)
    copies_meta = [
        remote(
            sent_meta, got_meta.at[i], send_meta_sem.at[i], recv_meta_sem.at[i], {"gz": dz}
        )
        for i, dz in enumerate(steps_z)
    ]
    for copy in copies_meta:
        copy.start()

    spans = (CAP_X, CAP_X, CAP_Z, CAP_Z, CAP_Y, CAP_Y)
    limit = jnp.zeros(lists_row.shape, jnp.int32)
    away = jnp.zeros(lists_row.shape, jnp.float32)
    start = 0
    for k, span in enumerate(spans):
        here = lane >= start
        limit = jnp.where(here, counts[0, k] + start, limit)
        away = jnp.where(here, float(GONE if k < 4 else (k - 3) * CELLS), away)
        start += span
    valid = lane < limit
    entries = lists_row[...]
    own_entry = valid & (entries < blocks)

    def table(ref, first, value, by_lane):
        number = first + lax.broadcasted_iota(jnp.int32, (ref.shape[0], lists_row.shape[1]), 0)
        hit = (lane if by_lane else entries) == number
        total = jnp.sum(jnp.where(hit, value, 0.0), axis=1, keepdims=True)
        ref[...] = jnp.broadcast_to(total, ref.shape)

    table(offsets, 0, jnp.where(valid, away, 0.0), False)
    y_slots = offsets_slot.at[pl.ds(2 * CAP_Z, 2 * CAP_Y)]
    table(y_slots, start_y, jnp.where(own_entry, away, float(GONE)), True)

    code = lax.broadcasted_iota(jnp.int32, (HALF, LANES), 0).astype(jnp.float32)

    def operands(v, cells, wanted):
        high = v.astype(jnp.bfloat16).astype(jnp.float32)
        both = jnp.concatenate([high, v - high], axis=0)
        part = jnp.floor(cells * (1.0 / HALF))
        inner = cells - part * HALF
        left = [
            jnp.concatenate(
                [
                    jnp.where(part == float(c * halves + h), both, 0.0).astype(jnp.bfloat16)
                    for c in group
                    for h in range(halves)
                ],
                axis=0,
            )
            for group in wanted
        ]
        right = jnp.where(code == inner, 1.0, 0.0).astype(jnp.bfloat16)
        return left, right

    def span_of(group):
        return pl.ds((group[0] - 1) * halves * 2 * rows, len(group) * halves * 2 * rows)

    def product(pairs, g):
        left = jnp.concatenate([a[g] for a, _ in pairs], axis=1)
        right = jnp.concatenate([b for _, b in pairs], axis=1)
        return lax.dot_general(
            left, right, (((1,), (1,)), ((), ())), preferred_element_type=jnp.float32
        )

    def own_slot(k, group):
        v, cells = own_block(jnp.minimum(lists[0, start_z + k], blocks - 1))
        return operands(v, cells + offsets_slot[pl.ds(k, 1), :], (group,))

    for side in range(2):
        first = 2 * CAP_Z + side * CAP_Y
        pairs = [own_slot(first + i, (1 + side,)) for i in range(CAP_Y)]
        acc[span_of((1 + side,)), :] = product(pairs, 0)

    for copy in copies_meta:
        copy.wait_recv()
    if len(steps_z) == 1:
        kind = got_meta[0, :1, :]
    else:
        kind = jnp.where(lane < start_z + CAP_Z, got_meta[1, :1, :], got_meta[0, :1, :] + 3.0)
    in_z = (lane >= start_z) & (lane < start_y)
    away = jnp.where(in_z, (kind + 3.0) * CELLS, away)
    table(offsets_x, blocks, jnp.where(valid, away, 0.0), False)
    z_slots = offsets_slot.at[pl.ds(0, 2 * CAP_Z)]
    table(z_slots, start_z, jnp.where(own_entry, away, float(GONE)), True)

    z_classes = tuple(range(3, len(classes)))
    pairs = [own_slot(i, z_classes) for i in range(2 * CAP_Z)]
    acc[span_of(z_classes), :] = product(pairs, 0)

    def unpacked(side, i):
        body = got_x[side, pl.ds(i * whole, whole), :]
        rest = got_x[side, pl.ds(CAP_X * whole + i * tail, tail), :]
        cells = got_x[side, pl.ds(CAP_X * field_count + i, 1), :]
        spare = jnp.broadcast_to(cells, (rows - field_count, LANES))
        return jnp.concatenate([body, rest, spare], axis=0), cells

    def got_blocks(side, wanted):
        base = (1 - side) * CAP_X
        pairs = []
        for i in range(CAP_X):
            v, cells = unpacked(side, i)
            pairs.append(operands(v, cells + offsets_x[pl.ds(base + i, 1), :], wanted))
        return pairs

    def wait_x(side):
        pltpu.make_async_remote_copy(
            src_ref=sent_x.at[pl.ds(side, 1)],
            dst_ref=got_x.at[pl.ds(side, 1)],
            send_sem=send_x_sem.at[side],
            recv_sem=recv_x_sem.at[side],
            device_id=target(moves_x[0]),
            device_id_type=pl.DeviceIdType.MESH,
        ).wait_recv()

    near = lax.rem(me["gx"], 2)
    wait_x(near)
    bound = tuple(range(1, len(classes)))
    acc[...] += product(got_blocks(near, (bound,)), 0)

    far = 1 - near
    wait_x(far)
    order = [c for c in bound if len(classes[c]) == 2]
    order += [c for c in bound if list(classes[c]) == ["gy"]]
    order += [c for c in bound if list(classes[c]) == ["gz"]]
    pairs = got_blocks(far, tuple((c,) for c in order))

    def packed(read):
        sums = [read(h, 0) + read(h, 1) for h in range(halves)]
        return [s[:whole] for s in sums] + [s[whole:field_count] for s in sums]

    def store(ref, c, pieces):
        for h in range(halves):
            ref[c, pl.ds(h * whole, whole), :] = pieces[h]
            ref[c, pl.ds(halves * whole + h * tail, tail), :] = pieces[halves + h]

    copies = {}
    for g, c in enumerate(order):
        total = acc[span_of((c,)), :] + product(pairs, g)

        def read(h, k):
            top = (h * 2 + k) * rows
            return total[top : top + rows]

        store(sent, c - 1, packed(read))
        copies[c] = remote(
            sent.at[c - 1],
            got.at[c - 1],
            send_sem.at[c - 1],
            recv_sem.at[c - 1],
            classes[c],
        )
        copies[c].start()

    acc_kept[...] = jnp.zeros_like(acc_kept)
    for side in range(2):
        base = (1 - side) * CAP_X
        pairs = []
        for i in range(CAP_X):
            v, cells = unpacked(side, i)
            pairs.append(operands(v, cells + offsets_x[pl.ds(base + i, 1), :], ((0,),)))
        acc_kept[...] += product(pairs, 0)

    def bin_own(g, carry):
        pairs = []
        for i in range(GROUP):
            b = g * GROUP + i
            v, cells = own_block(b)
            pairs.append(operands(v, cells + offsets[pl.ds(b, 1), :], ((0,),)))
        acc_kept[...] += product(pairs, 0)
        return carry

    lax.fori_loop(0, blocks // GROUP, bin_own, 0)

    total = packed(lambda h, k: acc_kept[pl.ds((h * 2 + k) * rows, rows), :])
    for c in [c for c in order if len(classes[c]) == 1] + [
        c for c in order if len(classes[c]) == 2
    ]:
        copies[c].wait_recv()
        for h in range(halves):
            total[h] = total[h] + got[c - 1, pl.ds(h * whole, whole), :]
            more = got[c - 1, pl.ds(halves * whole + h * tail, tail), :]
            total[halves + h] = total[halves + h] + more
    for h in range(halves):
        out_ref[:whole, pl.ds(h * HALF, HALF)] = total[h]
        out_ref[whole:, pl.ds(h * HALF, HALF)] = total[halves + h]
    for copy in copies_x + copies_meta + list(copies.values()):
        copy.wait_send()


def solution(mesh):
    sizes = {axis: mesh.shape[axis] for axis in AXES}

    def per_device(particle_fields, step_length, live_mask, dest_cell, block_counts, block_lists):
        field_count, particles = particle_fields.shape
        blocks = particles // LANES
        rows = (field_count + 1 + 7) // 8 * 8
        steps_z, classes = plan(sizes)
        sends = len(classes) - 1
        halves = CELLS // HALF
        sum_rows = (field_count * halves + 7) // 8 * 8
        packed_x = (CAP_X * (field_count + 1) + 7) // 8 * 8
        slots = 2 * CAP_Z + 2 * CAP_Y

        by_block = [a.reshape(blocks, LANES) for a in (step_length, live_mask, dest_cell)]
        any_space = pl.BlockSpec(memory_space=pl.ANY)
        f32 = jnp.float32
        return pl.pallas_call(
            functools.partial(migrate_kernel, sizes),
            out_shape=pltpu.VMEM((field_count, CELLS), f32),
            in_specs=[any_space] * 6,
            out_specs=pl.BlockSpec(memory_space=pltpu.VMEM),
            scratch_shapes=[
                pltpu.VMEM((field_count, particles), f32),
                pltpu.VMEM((blocks, LANES), f32),
                pltpu.VMEM((blocks, LANES), jnp.int32),
                pltpu.VMEM((blocks, LANES), jnp.int32),
                pltpu.VMEM((blocks, LANES), f32),
                pltpu.VMEM(((2 * CAP_X + 7) // 8 * 8, LANES), f32),
                pltpu.VMEM(((slots + 7) // 8 * 8, LANES), f32),
                pltpu.VMEM((2 * rows * halves, HALF), f32),
                pltpu.VMEM((2 * rows * halves * sends, HALF), f32),
                pltpu.VMEM((2, packed_x, LANES), f32),
                pltpu.VMEM((2, packed_x, LANES), f32),
                pltpu.VMEM((8, block_lists.shape[1]), f32),
                pltpu.VMEM((len(steps_z), 8, block_lists.shape[1]), f32),
                pltpu.VMEM((sends, sum_rows, HALF), f32),
                pltpu.VMEM((sends, sum_rows, HALF), f32),
                pltpu.SMEM(block_counts.shape, jnp.int32),
                pltpu.SMEM(block_lists.shape, jnp.int32),
                pltpu.VMEM(block_lists.shape, jnp.int32),
                pltpu.SemaphoreType.DMA((7,)),
                pltpu.SemaphoreType.DMA((2,)),
                pltpu.SemaphoreType.DMA((2,)),
                pltpu.SemaphoreType.DMA((len(steps_z),)),
                pltpu.SemaphoreType.DMA((len(steps_z),)),
                pltpu.SemaphoreType.DMA((sends,)),
                pltpu.SemaphoreType.DMA((sends,)),
            ],
            compiler_params=pltpu.CompilerParams(collective_id=0, has_side_effects=True),
        )(block_counts, block_lists, particle_fields, *by_block)

    placed = (
        P(None, AXES),
        P(AXES),
        P(AXES),
        P(AXES),
        P(AXES, None),
        P(AXES, None),
    )
    return jax.shard_map(
        per_device,
        mesh=mesh,
        in_specs=placed,
        out_specs=P(None, AXES),
        check_vma=False,
    )
```

time: 19.2 us -> 16.3 us (0.85)
  Pallas kernels: 18.4 us -> 15.5 us
    pallas_call x1, Pallas kernels: 18.4 us -> 15.5 us  [per_device(): pl.pallas_call(functools.partial(migrate_kernel, sizes), out_shape=pltpu....]
where the time goes in v2:
time: 16.3 us; the launch traced here: 16.1 us
  Pallas kernels  15.5 us (95%)
  local copies, waits for them, and re-layouts  0.62 us (4%)
    pallas_call x1, Pallas kernels, per_device(): pl.pallas_call(functools.partial(migrate_kernel, sizes), out_shape=pltpu....  15.5 us
    unnamed x1, local copies, waits for them, and re-layouts  0.62 us

profile of v2, /device:TPU:0, one launch (start us, length us, event | category | flops | bytes accessed | tf_op | source)
XLA Modules:
  0.0 16.1 jit_solution(17806193541418028124)
XLA Ops:
  0.0 15.5 %shard_map.64 = f32[20,512]{1,0:T(8,128)S(1)} custom-call(s32[1,6]{1,0:T(1,128)} %counts_hbm.1, s32[1,48]{1,0:T(1,128)} %lists_hbm.1, f32[20,8192]{1,0:T(8,128)} %fields_hbm.1, f32[64,128]{1,0:T(8,128)} %bitcast.3, s32[64,128]{1,0:T(8,128)} %bitcast.4, s32[64,128]{1,0:T(8,128)} %bitcast.5), custom_call_target="tpu_custom_call" | custom-call | tf_op jit(solution)/shard_map/pallas_call | solution.py:374
  15.5 0.6 %copy.8 = f32[20,512]{1,0:T(8,128)} copy(f32[20,512]{1,0:T(8,128)S(1)} %shard_map.64) | data formatting | bytes 81920

commit v3 on v2

v3 whole, which is shorter than its diff:
```python
import functools

import jax
import jax.numpy as jnp
from jax import lax
from jax.experimental import pallas as pl
from jax.experimental.pallas import tpu as pltpu
from jax.sharding import PartitionSpec as P

CELLS = 512
CAP_X = 6
CAP_Z = 6
CAP_Y = 12
LANES = 128
HALF = 256
GROUP = 8
GONE = 16
AXES = ("gx", "gy", "gz")


def plan(sizes):
    steps_z = (1,) if sizes["gz"] == 2 else (-1, 1)
    classes = [{}, {"gy": -1}, {"gy": 1}]
    for dz in steps_z:
        classes += [{"gz": dz}, {"gz": dz, "gy": -1}, {"gz": dz, "gy": 1}]
    return steps_z, classes


def migrate_kernel(
    sizes,
    counts_hbm,
    lists_hbm,
    fields_hbm,
    step_hbm,
    live_hbm,
    cell_hbm,
    out_ref,
    fields,
    step,
    live,
    cell,
    offsets,
    offsets_x,
    offsets_slot,
    acc_kept,
    acc,
    alone,
    sent_x,
    got_x,
    sent_meta,
    got_meta,
    sent,
    got,
    counts,
    lists,
    lists_row,
    load_sem,
    send_x_sem,
    recv_x_sem,
    send_meta_sem,
    recv_meta_sem,
    send_sem,
    recv_sem,
    ready,
):
    steps_z, classes = plan(sizes)
    field_count = fields_hbm.shape[0]
    rows = (field_count + 1 + 7) // 8 * 8
    whole = field_count // 8 * 8
    tail = field_count - whole
    blocks = step.shape[0]
    halves = CELLS // HALF
    start_z, start_y = 2 * CAP_X, 2 * CAP_X + 2 * CAP_Z

    me = {axis: lax.axis_index(axis) for axis in AXES}

    def target(moves):
        return {a: lax.rem(me[a] + sizes[a] + d, sizes[a]) for a, d in moves.items()}

    def remote(src, dst, send, recv, moves):
        return pltpu.make_async_remote_copy(
            src_ref=src,
            dst_ref=dst,
            send_sem=send,
            recv_sem=recv,
            device_id=target(moves),
            device_id_type=pl.DeviceIdType.MESH,
        )

    loads = [
        pltpu.make_async_copy(src, dst, load_sem.at[i])
        for i, (src, dst) in enumerate(
            [
                (counts_hbm, counts),
                (lists_hbm, lists),
                (lists_hbm, lists_row),
                (step_hbm, step),
                (live_hbm, live),
                (cell_hbm, cell),
                (fields_hbm, fields),
            ]
        )
    ]
    for load in loads:
        load.start()

    moves_x = ({"gx": -1}, {"gx": 1})
    partners = {0: [], -1: [], 1: []}
    seen = set()
    for moves in list(moves_x) + classes[1:]:
        place = tuple(moves.get(a, 0) % sizes[a] for a in AXES)
        if place not in seen:
            seen.add(place)
            partners[moves.get("gy", 0) if sizes["gy"] > 2 else 0].append(moves)
    greets = {-1: me["gy"] == 0, 1: me["gy"] < sizes["gy"] - 1}
    barrier = pltpu.get_barrier_semaphore()

    def signal(semaphore, group):
        for moves in group:
            pl.semaphore_signal(
                semaphore, inc=1, device_id=target(moves), device_id_type=pl.DeviceIdType.MESH
            )

    signal(barrier, partners[0])
    for dy in (-1, 1):
        pl.when(greets[dy])(functools.partial(signal, barrier, partners[dy]))

    expected = len(partners[0])
    for dy in (-1, 1):
        expected += jnp.logical_not(greets[dy]).astype(jnp.int32) * len(partners[dy])

    for load in loads[:3]:
        load.wait()

    lane = lax.broadcasted_iota(jnp.int32, lists_row.shape, 1)
    z_number = blocks + 2 * CAP_X + jnp.where(
        lane < start_z + CAP_Z, lane - start_z + CAP_Z, lane - start_z - CAP_Z
    )
    onward = jnp.zeros(lists_row.shape, jnp.float32)
    for k in range(2 * CAP_Y):
        side, i = k // CAP_Y, k % CAP_Y
        count = jnp.full(lists_row.shape, counts[0, 4 + side])
        hit = (z_number == lists[0, start_y + k]) & (count > i)
        onward = jnp.where(hit, float(1 + side), onward)
    sent_meta[...] = jnp.broadcast_to(onward, sent_meta.shape)

    pl.semaphore_wait(barrier, expected)

    copies_meta = [
        remote(
            sent_meta, got_meta.at[i], send_meta_sem.at[i], recv_meta_sem.at[i], {"gz": dz}
        )
        for i, dz in enumerate(steps_z)
    ]
    for copy in copies_meta:
        copy.start()
    for dy in (-1, 1):
        heard = ready.at[(1 - dy) // 2]
        pl.when(jnp.logical_not(greets[dy]))(functools.partial(signal, heard, partners[dy]))

    for load in loads[3:]:
        load.wait()

    first_row = lax.broadcasted_iota(jnp.int32, (8, LANES), 0)

    def own_block(e):
        v = fields[:, pl.ds(e * LANES, LANES)]
        top = v[:8]
        pace = step[pl.ds(e, 1), :]
        top = top + jnp.where(first_row < 3, pace * pltpu.roll(top, 5, 0), 0.0)
        v = jnp.concatenate([top, v[8:]], axis=0)
        v = v * live[pl.ds(e, 1), :].astype(jnp.float32)
        where_to = cell[pl.ds(e, 1), :].astype(jnp.float32)
        return jnp.concatenate([v, v[whole:]], axis=0), where_to

    for slot in range(2 * CAP_X):
        block, where_to = own_block(jnp.minimum(lists[0, slot], blocks - 1))
        side, i = slot // CAP_X, slot % CAP_X
        count = jnp.full((rows, LANES), counts[0, side])
        block = jnp.where(count > i, block, 0.0)
        where_to = jnp.where(count[:1] > i, where_to, 0.0)
        sent_x[side, pl.ds(i * whole, whole), :] = block[:whole]
        sent_x[side, pl.ds(CAP_X * whole + i * tail, tail), :] = block[whole:field_count]
        sent_x[side, pl.ds(CAP_X * field_count + i, 1), :] = where_to

    def copy_x(side):
        return [
            remote(
                sent_x.at[pl.ds(s, 1)],
                got_x.at[pl.ds(s, 1)],
                send_x_sem.at[s],
                recv_x_sem.at[s],
                moves_x[s],
            )
            for s in side
        ]

    copies_x = copy_x((0, 1))
    for copy in copies_x:
        copy.start()

    spans = (CAP_X, CAP_X, CAP_Z, CAP_Z, CAP_Y, CAP_Y)
    limit = jnp.zeros(lists_row.shape, jnp.int32)
    away = jnp.zeros(lists_row.shape, jnp.float32)
    start = 0
    for k, span in enumerate(spans):
        here = lane >= start
        limit = jnp.where(here, counts[0, k] + start, limit)
        away = jnp.where(here, float(GONE if k < 4 else k - 3), away)
        start += span
    valid = lane < limit
    entries = lists_row[...]
    own_entry = valid & (entries < blocks)

    def table(ref, first, value, by_lane):
        number = first + lax.broadcasted_iota(jnp.int32, (ref.shape[0], lists_row.shape[1]), 0)
        hit = (lane if by_lane else entries) == number
        total = jnp.sum(jnp.where(hit, value, 0.0), axis=1, keepdims=True)
        ref[...] = jnp.broadcast_to(total, ref.shape)

    table(offsets, 0, jnp.where(valid, away, 0.0), False)
    y_slots = offsets_slot.at[pl.ds(2 * CAP_Z, 2 * CAP_Y)]
    table(y_slots, start_y, jnp.where(own_entry, away, float(GONE)), True)

    pack = 2 * 8
    bf16 = jnp.bfloat16
    row16 = lax.broadcasted_iota(jnp.int32, (pack, LANES), 0)
    code = row16.astype(jnp.float32)
    second = jnp.where(row16 >= 8, 1.0, 0.0)

    zero = jnp.zeros((pack, LANES), bf16)
    one = jnp.ones((pack, LANES), bf16)

    def prepared(v, cells):
        body, end = v[:whole], v[whole:]
        high = body.astype(bf16)
        low = (body - high.astype(jnp.float32)).astype(bf16)
        end_high = end.astype(bf16).astype(jnp.float32)
        end = jnp.where(first_row < tail, end_high, end - end_high)
        end = jnp.concatenate([end, end], axis=0).astype(bf16)
        part = jnp.floor(cells * (1.0 / HALF))
        ahead = (jnp.broadcast_to(cells - part * HALF, (pack, LANES)) - code).astype(bf16)
        right = [
            jnp.where(ahead == jnp.full((pack, LANES), k, bf16), one, zero)
            for k in range(0, HALF, pack)
        ]
        return high, low, end, part, jnp.concatenate(right, axis=0)

    def masked(block, kind, group):
        high, low, end, part, right = block
        part = jnp.broadcast_to(part + kind * halves, (pack, LANES))
        part_end = (part - second).astype(bf16)
        part = part.astype(bf16)
        left = []
        for c in group:
            for h in range(halves):
                here = part == jnp.full((pack, LANES), c * halves + h, bf16)
                left += [jnp.where(here, high, zero), jnp.where(here, low, zero)]
            here = part_end == jnp.full((pack, LANES), c * halves, bf16)
            left.append(jnp.where(here, end, zero))
        return jnp.concatenate(left, axis=0), right

    each = 2 * whole * halves + pack

    def span_of(group):
        return pl.ds((group[0] - 1) * each, len(group) * each)

    def product(pairs):
        left = jnp.concatenate([a for a, _ in pairs], axis=1)
        right = jnp.concatenate([b for _, b in pairs], axis=1)
        return lax.dot_general(
            left, right, (((1,), (1,)), ((), ())), preferred_element_type=jnp.float32
        )

    top_rows = lax.broadcasted_iota(jnp.int32, (8, HALF), 0) < tail

    def packed(r):
        out = []
        for h in range(halves):
            high = 2 * h * whole
            out.append(r[high : high + whole] + r[high + whole : high + 2 * whole])
        ends = [r[2 * halves * whole + 8 * h :][:8] for h in range(halves)]
        ends = [e + pltpu.roll(e, tail, 0) for e in ends]
        return out + [jnp.where(top_rows, ends[0], ends[1])]

    def own_slot(k):
        return prepared(*own_block(jnp.minimum(lists[0, start_z + k], blocks - 1)))

    def slot_kind(k):
        return offsets_slot[pl.ds(k, 1), :]

    for side in range(2):
        first = 2 * CAP_Z + side * CAP_Y
        slots = range(first, first + CAP_Y)
        pairs = [masked(own_slot(k), slot_kind(k), (1 + side,)) for k in slots]
        acc[span_of((1 + side,)), :] = product(pairs)

    def unpacked(side, i):
        body = got_x[side, pl.ds(i * whole, whole), :]
        rest = got_x[side, pl.ds(CAP_X * whole + i * tail, tail), :]
        cells = got_x[side, pl.ds(CAP_X * field_count + i, 1), :]
        return jnp.concatenate([body, rest, rest], axis=0), cells

    def wait_x(side):
        pltpu.make_async_remote_copy(
            src_ref=sent_x.at[pl.ds(side, 1)],
            dst_ref=got_x.at[pl.ds(side, 1)],
            send_sem=send_x_sem.at[side],
            recv_sem=recv_x_sem.at[side],
            device_id=target(moves_x[0]),
            device_id_type=pl.DeviceIdType.MESH,
        ).wait_recv()

    bound = tuple(range(1, len(classes)))
    y_classes, z_classes = bound[:2], bound[2:]
    near = lax.rem(me["gx"], 2)
    far = 1 - near

    def got_kind(ref, side, i):
        base = (1 - side) * CAP_X
        return ref[pl.ds(base + i, 1), :]

    def block_sums(ref, i, block):
        plain = masked(block, jnp.zeros((1, LANES), jnp.float32), (0,))
        ref[i] = jnp.concatenate(packed(product([plain])), axis=0)

    for k in range(2 * CAP_Z):
        block_sums(alone, k, own_slot(k))
    wait_x(near)
    near_blocks = [prepared(*unpacked(near, i)) for i in range(CAP_X)]
    for i, block in enumerate(near_blocks):
        block_sums(alone, 2 * CAP_Z + i, block)
    kinds = [got_kind(offsets.at[pl.ds(blocks, 2 * CAP_X)], near, i) for i in range(CAP_X)]
    pairs = [masked(v, kind, y_classes) for v, kind in zip(near_blocks, kinds)]
    acc[...] += product(pairs)

    for copy in copies_meta:
        copy.wait_recv()
    if len(steps_z) == 1:
        kind = got_meta[0, :1, :]
    else:
        kind = jnp.where(lane < start_z + CAP_Z, got_meta[1, :1, :], got_meta[0, :1, :] + 3.0)
    in_z = (lane >= start_z) & (lane < start_y)
    away = jnp.where(in_z, kind + 3.0, away)
    table(offsets_x, blocks, jnp.where(valid, away, 0.0), False)
    z_slots = offsets_slot.at[pl.ds(0, 2 * CAP_Z)]
    table(z_slots, start_z, jnp.where(own_entry, away, float(GONE)), True)

    kinds = [slot_kind(k) for k in range(2 * CAP_Z)]
    kinds += [got_kind(offsets_x, near, i) for i in range(CAP_X)]
    kinds = [jnp.concatenate([kind] * (HALF // LANES), axis=1) for kind in kinds]
    for c in z_classes:
        sent[c - 1] = sum(
            jnp.where(kind == float(c), alone[k], 0.0) for k, kind in enumerate(kinds)
        )

    wait_x(far)
    pairs = []
    for i in range(CAP_X):
        pairs.append(masked(prepared(*unpacked(far, i)), got_kind(offsets_x, far, i), bound))
    sums = product(pairs)
    for c in bound:
        total = sums[(c - 1) * each : c * each]
        if c in y_classes:
            total = total + acc[span_of((c,)), :]
        total = jnp.concatenate(packed(total), axis=0)
        sent[c - 1] = total + sent[c - 1] if c in z_classes else total

    def message(c, moves):
        return remote(sent.at[c], got.at[c], send_sem.at[c], recv_sem.at[c], moves)

    for dy in (-1, 1):
        heard = functools.partial(pl.semaphore_wait, ready.at[(1 + dy) // 2], len(partners[dy]))
        if partners[dy]:
            pl.when(greets[dy])(heard)
    side = jnp.where(me["gy"] == 0, 0, 1)
    copies = []
    for s in (side, 1 - side):
        for q, dz in enumerate(steps_z):
            copies.append(message(3 * q + 3 + s, {"gz": dz, "gy": 2 * s - 1}))
        copies.append(message(s, {"gy": 2 * s - 1}))
    for q, dz in enumerate(steps_z):
        copies.append(message(3 * q + 2, {"gz": dz}))
    for copy in copies:
        copy.start()

    acc_kept[...] = jnp.zeros_like(acc_kept)
    for side in range(2):
        pairs = []
        for i in range(CAP_X):
            pairs.append(masked(prepared(*unpacked(side, i)), got_kind(offsets_x, side, i), (0,)))
        acc_kept[...] += product(pairs)

    def bin_own(g, carry):
        pairs = []
        for i in range(GROUP):
            b = g * GROUP + i
            pairs.append(masked(prepared(*own_block(b)), offsets[pl.ds(b, 1), :], (0,)))
        acc_kept[...] += product(pairs)
        return carry

    lax.fori_loop(0, blocks // GROUP, bin_own, 0)

    total = jnp.concatenate(packed(acc_kept[...]), axis=0)
    for c in (3, 6, 1, 2, 4, 5, 7, 8):
        if c in bound:
            message(c - 1, classes[c]).wait_recv()
            total = total + got[c - 1]
    for h in range(halves):
        here = pl.ds(h * HALF, HALF)
        out_ref[:whole, here] = total[h * whole : (h + 1) * whole]
        last = halves * whole + h * tail
        out_ref[whole:, here] = total[last : last + tail]
    for copy in copies_x + copies_meta + copies:
        copy.wait_send()


def solution(mesh):
    sizes = {axis: mesh.shape[axis] for axis in AXES}

    def per_device(particle_fields, step_length, live_mask, dest_cell, block_counts, block_lists):
        field_count, particles = particle_fields.shape
        blocks = particles // LANES
        rows = (field_count + 1 + 7) // 8 * 8
        steps_z, classes = plan(sizes)
        sends = len(classes) - 1
        halves = CELLS // HALF
        sum_rows = (field_count * halves + 7) // 8 * 8
        packed_x = (CAP_X * (field_count + 1) + 7) // 8 * 8
        slots = 2 * CAP_Z + 2 * CAP_Y
        each = 2 * (field_count // 8 * 8) * halves + 16

        by_block = [a.reshape(blocks, LANES) for a in (step_length, live_mask, dest_cell)]
        any_space = pl.BlockSpec(memory_space=pl.ANY)
        f32 = jnp.float32
        return pl.pallas_call(
            functools.partial(migrate_kernel, sizes),
            out_shape=pltpu.VMEM((field_count, CELLS), f32),
            in_specs=[any_space] * 6,
            out_specs=pl.BlockSpec(memory_space=pltpu.VMEM),
            scratch_shapes=[
                pltpu.VMEM((field_count, particles), f32),
                pltpu.VMEM((blocks, LANES), f32),
                pltpu.VMEM((blocks, LANES), jnp.int32),
                pltpu.VMEM((blocks, LANES), jnp.int32),
                pltpu.VMEM((blocks + (2 * CAP_X + 7) // 8 * 8, LANES), f32),
                pltpu.VMEM(((2 * CAP_X + 7) // 8 * 8, LANES), f32),
                pltpu.VMEM(((slots + 7) // 8 * 8, LANES), f32),
                pltpu.VMEM((each, HALF), f32),
                pltpu.VMEM((each * 2, HALF), f32),
                pltpu.VMEM((2 * CAP_Z + CAP_X, sum_rows, HALF), f32),
                pltpu.VMEM((2, packed_x, LANES), f32),
                pltpu.VMEM((2, packed_x, LANES), f32),
                pltpu.VMEM((8, block_lists.shape[1]), f32),
                pltpu.VMEM((len(steps_z), 8, block_lists.shape[1]), f32),
                pltpu.VMEM((sends, sum_rows, HALF), f32),
                pltpu.VMEM((sends, sum_rows, HALF), f32),
                pltpu.SMEM(block_counts.shape, jnp.int32),
                pltpu.SMEM(block_lists.shape, jnp.int32),
                pltpu.VMEM(block_lists.shape, jnp.int32),
                pltpu.SemaphoreType.DMA((7,)),
                pltpu.SemaphoreType.DMA((2,)),
                pltpu.SemaphoreType.DMA((2,)),
                pltpu.SemaphoreType.DMA((len(steps_z),)),
                pltpu.SemaphoreType.DMA((len(steps_z),)),
                pltpu.SemaphoreType.DMA((sends,)),
                pltpu.SemaphoreType.DMA((sends,)),
                pltpu.SemaphoreType.REGULAR((2,)),
            ],
            compiler_params=pltpu.CompilerParams(collective_id=0, has_side_effects=True),
        )(block_counts, block_lists, particle_fields, *by_block)

    placed = (
        P(None, AXES),
        P(AXES),
        P(AXES),
        P(AXES),
        P(AXES, None),
        P(AXES, None),
    )
    return jax.shard_map(
        per_device,
        mesh=mesh,
        in_specs=placed,
        out_specs=P(None, AXES),
        check_vma=False,
    )
```

time: 16.3 us -> 14.2 us (0.87)
  Pallas kernels: 15.5 us -> 13.4 us
    pallas_call x1, Pallas kernels: 15.5 us -> 13.4 us  [per_device(): pl.pallas_call(functools.partial(migrate_kernel, sizes), out_shape=pltpu....]
where the time goes in v3:
time: 14.2 us; the launch traced here: 14.1 us
  Pallas kernels  13.4 us (94%)
  local copies, waits for them, and re-layouts  0.62 us (4%)
    pallas_call x1, Pallas kernels, per_device(): pl.pallas_call(functools.partial(migrate_kernel, sizes), out_shape=pltpu....  13.4 us
    unnamed x1, local copies, waits for them, and re-layouts  0.62 us

profile of v3, /device:TPU:0, one launch (start us, length us, event | category | flops | bytes accessed | tf_op | source)
XLA Modules:
  0.0 14.1 jit_solution(9397255935697351507)
XLA Ops:
  0.0 13.4 %shard_map.64 = f32[20,512]{1,0:T(8,128)S(1)} custom-call(s32[1,6]{1,0:T(1,128)} %counts_hbm.1, s32[1,48]{1,0:T(1,128)} %lists_hbm.1, f32[20,8192]{1,0:T(8,128)} %fields_hbm.1, f32[64,128]{1,0:T(8,128)} %bitcast.3, s32[64,128]{1,0:T(8,128)} %bitcast.4, s32[64,128]{1,0:T(8,128)} %bitcast.5), custom_call_target="tpu_custom_call" | custom-call | tf_op jit(solution)/shard_map/pallas_call | solution.py:436
  13.4 0.6 %copy.8 = f32[20,512]{1,0:T(8,128)} copy(f32[20,512]{1,0:T(8,128)S(1)} %shard_map.64) | data formatting | bytes 81920

commit v4 on v3

--- a/solution.py
+++ b/solution.py
@@ -283,6 +283,12 @@
         ends = [e + pltpu.roll(e, tail, 0) for e in ends]
         return out + [jnp.where(top_rows, ends[0], ends[1])]
 
+    def spread(blocks, kinds, group):
+        half = len(blocks) // 2
+        minus = [(-high, -low, -end, *rest) for high, low, end, *rest in blocks[half:]]
+        pairs = [masked(v, kind, group) for v, kind in zip(blocks[:half] + minus, kinds)]
+        return product(pairs[:half]) - product(pairs[half:])
+
     def own_slot(k):
         return prepared(*own_block(jnp.minimum(lists[0, start_z + k], blocks - 1)))
 
@@ -331,8 +337,7 @@
     for i, block in enumerate(near_blocks):
         block_sums(alone, 2 * CAP_Z + i, block)
     kinds = [got_kind(offsets.at[pl.ds(blocks, 2 * CAP_X)], near, i) for i in range(CAP_X)]
-    pairs = [masked(v, kind, y_classes) for v, kind in zip(near_blocks, kinds)]
-    acc[...] += product(pairs)
+    acc[...] += spread(near_blocks, kinds, y_classes)
 
     for copy in copies_meta:
         copy.wait_recv()
@@ -354,54 +359,65 @@
             jnp.where(kind == float(c), alone[k], 0.0) for k, kind in enumerate(kinds)
         )
 
+    acc_kept[...] = jnp.zeros_like(acc_kept)
+
+    def bin_own(g, carry):
+        numbers = [g * GROUP + i for i in range(GROUP)]
+        kinds = [offsets[pl.ds(b, 1), :] for b in numbers]
+        acc_kept[...] += spread([prepared(*own_block(b)) for b in numbers], kinds, (0,))
+        return carry
+
     wait_x(far)
-    pairs = []
-    for i in range(CAP_X):
-        pairs.append(masked(prepared(*unpacked(far, i)), got_kind(offsets_x, far, i), bound))
-    sums = product(pairs)
-    for c in bound:
-        total = sums[(c - 1) * each : c * each]
-        if c in y_classes:
-            total = total + acc[span_of((c,)), :]
-        total = jnp.concatenate(packed(total), axis=0)
-        sent[c - 1] = total + sent[c - 1] if c in z_classes else total
+    far_blocks = [prepared(*unpacked(far, i)) for i in range(CAP_X)]
+
+    def finish(group):
+        sums = spread(far_blocks, [got_kind(offsets_x, far, i) for i in range(CAP_X)], group)
+        for g, c in enumerate(group):
+            total = sums[g * each : (g + 1) * each]
+            if c in y_classes:
+                total = total + acc[span_of((c,)), :]
+            total = jnp.concatenate(packed(total), axis=0)
+            sent[c - 1] = total + sent[c - 1] if c in z_classes else total
 
     def message(c, moves):
         return remote(sent.at[c], got.at[c], send_sem.at[c], recv_sem.at[c], moves)
 
+    side = jnp.where(me["gy"] == sizes["gy"] - 1, 1, 0)
+    across = [c for c in bound if len(classes[c]) == 2]
+    finish(across)
     for dy in (-1, 1):
         heard = functools.partial(pl.semaphore_wait, ready.at[(1 + dy) // 2], len(partners[dy]))
         if partners[dy]:
             pl.when(greets[dy])(heard)
-    side = jnp.where(me["gy"] == 0, 0, 1)
-    copies = []
-    for s in (side, 1 - side):
-        for q, dz in enumerate(steps_z):
-            copies.append(message(3 * q + 3 + s, {"gz": dz, "gy": 2 * s - 1}))
-        copies.append(message(s, {"gy": 2 * s - 1}))
+    first = [
+        message(3 * q + 3 + side, {"gz": dz, "gy": 2 * side - 1}) for q, dz in enumerate(steps_z)
+    ]
+    held = jnp.where(near == 1, 1, 0)
+    lax.fori_loop(0, held, bin_own, 0)
+    for copy in first:
+        copy.start()
+    finish([c for c in bound if c not in across])
+    rest = [message(side, {"gy": 2 * side - 1})]
     for q, dz in enumerate(steps_z):
-        copies.append(message(3 * q + 2, {"gz": dz}))
-    for copy in copies:
+        rest.append(message(3 * q + 4 - side, {"gz": dz, "gy": 1 - 2 * side}))
+    rest.append(message(1 - side, {"gy": 1 - 2 * side}))
+    for q, dz in enumerate(steps_z):
+        rest.append(message(3 * q + 2, {"gz": dz}))
+    for copy in rest:
         copy.start()
-
-    acc_kept[...] = jnp.zeros_like(acc_kept)
+    copies = first + rest
+
     for side in range(2):
         pairs = []
         for i in range(CAP_X):
             pairs.append(masked(prepared(*unpacked(side, i)), got_kind(offsets_x, side, i), (0,)))
         acc_kept[...] += product(pairs)
 
-    def bin_own(g, carry):
-        pairs = []
-        for i in range(GROUP):
-            b = g * GROUP + i
-            pairs.append(masked(prepared(*own_block(b)), offsets[pl.ds(b, 1), :], (0,)))
-        acc_kept[...] += product(pairs)
-        return carry
-
-    lax.fori_loop(0, blocks // GROUP, bin_own, 0)
+    lax.fori_loop(held, blocks // GROUP, bin_own, 0)
 
     total = jnp.concatenate(packed(acc_kept[...]), axis=0)
+    for copy in copies_x + copies_meta + copies:
+        copy.wait_send()
     for c in (3, 6, 1, 2, 4, 5, 7, 8):
         if c in bound:
             message(c - 1, classes[c]).wait_recv()
@@ -411,8 +427,6 @@
         out_ref[:whole, here] = total[h * whole : (h + 1) * whole]
         last = halves * whole + h * tail
         out_ref[whole:, here] = total[last : last + tail]
-    for copy in copies_x + copies_meta + copies:
-        copy.wait_send()
 
 
 def solution(mesh):

time: 14.2 us -> 13.8 us (0.972)
  Pallas kernels: 13.4 us -> 12.9 us
    pallas_call x1, Pallas kernels: 13.4 us -> 12.9 us  [per_device(): pl.pallas_call(functools.partial(migrate_kernel, sizes), out_shape=pltpu....]
where the time goes in v4:
time: 13.8 us; the launch traced here: 13.6 us
  Pallas kernels  12.9 us (93%)
  local copies, waits for them, and re-layouts  0.62 us (4%)
    pallas_call x1, Pallas kernels, per_device(): pl.pallas_call(functools.partial(migrate_kernel, sizes), out_shape=pltpu....  12.9 us
    unnamed x1, local copies, waits for them, and re-layouts  0.62 us

profile of v4, /device:TPU:0, one launch (start us, length us, event | category | flops | bytes accessed | tf_op | source)
XLA Modules:
  0.0 13.6 jit_solution(12063859152659375962)
XLA Ops:
  0.0 12.9 %shard_map.64 = f32[20,512]{1,0:T(8,128)S(1)} custom-call(s32[1,6]{1,0:T(1,128)} %counts_hbm.1, s32[1,48]{1,0:T(1,128)} %lists_hbm.1, f32[20,8192]{1,0:T(8,128)} %fields_hbm.1, f32[64,128]{1,0:T(8,128)} %bitcast.3, s32[64,128]{1,0:T(8,128)} %bitcast.4, s32[64,128]{1,0:T(8,128)} %bitcast.5), custom_call_target="tpu_custom_call" | custom-call | tf_op jit(solution)/shard_map/pallas_call | solution.py:450
  12.9 0.6 %copy.8 = f32[20,512]{1,0:T(8,128)} copy(f32[20,512]{1,0:T(8,128)S(1)} %shard_map.64) | data formatting | bytes 81920

commit v5 on v4

--- a/solution.py
+++ b/solution.py
@@ -35,7 +35,8 @@
     live_hbm,
     cell_hbm,
     out_ref,
-    fields,
+    bodies,
+    ends,
     step,
     live,
     cell,
@@ -96,8 +97,9 @@
                 (lists_hbm, lists_row),
                 (step_hbm, step),
                 (live_hbm, live),
+                (fields_hbm.at[pl.ds(0, whole)], bodies),
                 (cell_hbm, cell),
-                (fields_hbm, fields),
+                (fields_hbm.at[pl.ds(whole, tail)], ends),
             ]
         )
     ]
@@ -158,45 +160,60 @@
         heard = ready.at[(1 - dy) // 2]
         pl.when(jnp.logical_not(greets[dy]))(functools.partial(signal, heard, partners[dy]))
 
-    for load in loads[3:]:
-        load.wait()
-
     first_row = lax.broadcasted_iota(jnp.int32, (8, LANES), 0)
 
+    def columns(e):
+        return pl.ds(e * LANES, LANES)
+
+    def alive(e):
+        return live[pl.ds(e, 1), :].astype(jnp.float32)
+
+    def own_body(e):
+        v = bodies[:, columns(e)]
+        top = v[:8]
+        top = top + jnp.where(first_row < 3, step[pl.ds(e, 1), :] * pltpu.roll(top, 5, 0), 0.0)
+        return jnp.concatenate([top, v[8:]], axis=0) * alive(e)
+
+    def own_end(e):
+        return ends[:, columns(e)] * alive(e), cell[pl.ds(e, 1), :].astype(jnp.float32)
+
     def own_block(e):
-        v = fields[:, pl.ds(e * LANES, LANES)]
-        top = v[:8]
-        pace = step[pl.ds(e, 1), :]
-        top = top + jnp.where(first_row < 3, pace * pltpu.roll(top, 5, 0), 0.0)
-        v = jnp.concatenate([top, v[8:]], axis=0)
-        v = v * live[pl.ds(e, 1), :].astype(jnp.float32)
-        where_to = cell[pl.ds(e, 1), :].astype(jnp.float32)
-        return jnp.concatenate([v, v[whole:]], axis=0), where_to
-
-    for slot in range(2 * CAP_X):
-        block, where_to = own_block(jnp.minimum(lists[0, slot], blocks - 1))
+        end, where_to = own_end(e)
+        return jnp.concatenate([own_body(e), end, end], axis=0), where_to
+
+    def leaving(slot):
         side, i = slot // CAP_X, slot % CAP_X
-        count = jnp.full((rows, LANES), counts[0, side])
-        block = jnp.where(count > i, block, 0.0)
-        where_to = jnp.where(count[:1] > i, where_to, 0.0)
-        sent_x[side, pl.ds(i * whole, whole), :] = block[:whole]
-        sent_x[side, pl.ds(CAP_X * whole + i * tail, tail), :] = block[whole:field_count]
-        sent_x[side, pl.ds(CAP_X * field_count + i, 1), :] = where_to
-
-    def copy_x(side):
+        return side, i, jnp.minimum(lists[0, slot], blocks - 1), counts[0, side]
+
+    def copies_of(first, count):
+        part = pl.ds(first, count)
         return [
             remote(
-                sent_x.at[pl.ds(s, 1)],
-                got_x.at[pl.ds(s, 1)],
-                send_x_sem.at[s],
-                recv_x_sem.at[s],
-                moves_x[s],
+                sent_x.at[s, part], got_x.at[s, part], send_x_sem, recv_x_sem.at[s], moves_x[s]
             )
-            for s in side
+            for s in range(2)
         ]
 
-    copies_x = copy_x((0, 1))
-    for copy in copies_x:
+    body_rows = CAP_X * whole
+    copies_x = copies_of(0, body_rows) + copies_of(body_rows, sent_x.shape[1] - body_rows)
+    for load in loads[3:6]:
+        load.wait()
+    for slot in range(2 * CAP_X):
+        side, i, e, count = leaving(slot)
+        block = jnp.where(jnp.full((whole, LANES), count) > i, own_body(e), 0.0)
+        sent_x[side, pl.ds(i * whole, whole), :] = block
+    for copy in copies_x[:2]:
+        copy.start()
+    for load in loads[6:]:
+        load.wait()
+    for slot in range(2 * CAP_X):
+        side, i, e, count = leaving(slot)
+        end, where_to = own_end(e)
+        taken = jnp.full((tail, LANES), count) > i
+        sent_x[side, pl.ds(body_rows + i * tail, tail), :] = jnp.where(taken, end, 0.0)
+        where_to = jnp.where(taken[:1], where_to, 0.0)
+        sent_x[side, pl.ds(CAP_X * field_count + i, 1), :] = where_to
+    for copy in copies_x[2:]:
         copy.start()
 
     spans = (CAP_X, CAP_X, CAP_Z, CAP_Z, CAP_Y, CAP_Y)
@@ -246,6 +263,9 @@
         ]
         return high, low, end, part, jnp.concatenate(right, axis=0)
 
+    def level(number):
+        return jnp.full((pack, LANES), number, jnp.float32).astype(bf16)
+
     def masked(block, kind, group):
         high, low, end, part, right = block
         part = jnp.broadcast_to(part + kind * halves, (pack, LANES))
@@ -254,9 +274,9 @@
         left = []
         for c in group:
             for h in range(halves):
-                here = part == jnp.full((pack, LANES), c * halves + h, bf16)
+                here = part == level(c * halves + h)
                 left += [jnp.where(here, high, zero), jnp.where(here, low, zero)]
-            here = part_end == jnp.full((pack, LANES), c * halves, bf16)
+            here = part_end == level(c * halves)
             left.append(jnp.where(here, end, zero))
         return jnp.concatenate(left, axis=0), right
 
@@ -311,7 +331,7 @@
         pltpu.make_async_remote_copy(
             src_ref=sent_x.at[pl.ds(side, 1)],
             dst_ref=got_x.at[pl.ds(side, 1)],
-            send_sem=send_x_sem.at[side],
+            send_sem=send_x_sem,
             recv_sem=recv_x_sem.at[side],
             device_id=target(moves_x[0]),
             device_id_type=pl.DeviceIdType.MESH,
@@ -337,7 +357,10 @@
     for i, block in enumerate(near_blocks):
         block_sums(alone, 2 * CAP_Z + i, block)
     kinds = [got_kind(offsets.at[pl.ds(blocks, 2 * CAP_X)], near, i) for i in range(CAP_X)]
-    acc[...] += spread(near_blocks, kinds, y_classes)
+    more = spread(near_blocks, kinds, y_classes)
+    for c in y_classes:
+        total = acc[span_of((c,)), :] + more[(c - 1) * each : c * each]
+        sent[c - 1] = jnp.concatenate(packed(total), axis=0)
 
     for copy in copies_meta:
         copy.wait_recv()
@@ -373,38 +396,46 @@
     def finish(group):
         sums = spread(far_blocks, [got_kind(offsets_x, far, i) for i in range(CAP_X)], group)
         for g, c in enumerate(group):
-            total = sums[g * each : (g + 1) * each]
-            if c in y_classes:
-                total = total + acc[span_of((c,)), :]
-            total = jnp.concatenate(packed(total), axis=0)
-            sent[c - 1] = total + sent[c - 1] if c in z_classes else total
+            pieces = packed(sums[g * each : (g + 1) * each])
+            sent[c - 1] += jnp.concatenate(pieces, axis=0)
 
     def message(c, moves):
-        return remote(sent.at[c], got.at[c], send_sem.at[c], recv_sem.at[c], moves)
+        return remote(sent.at[c - 1], got.at[c - 1], send_sem, recv_sem, moves)
 
     side = jnp.where(me["gy"] == sizes["gy"] - 1, 1, 0)
-    across = [c for c in bound if len(classes[c]) == 2]
-    finish(across)
+    along, across = (1, {}), [(3 * q + 4, {"gz": dz}) for q, dz in enumerate(steps_z)]
+    straight = [(3 * q + 3, {"gz": dz}) for q, dz in enumerate(steps_z)]
+    if len(steps_z) == 1:
+        lead = jnp.where(me["gz"] == 0, 0, 1)
+        ahead = [(1 + 3 * lead, {"gz": lead})]
+        behind = [(4 - 3 * lead, {"gz": 1 - lead})]
+    else:
+        ahead, behind = across, [along]
+
+    def on_side(group, s):
+        return [message(c + s, moves | {"gy": 2 * s - 1}) for c, moves in group]
+
+    finish([c + side for c, _ in ahead])
     for dy in (-1, 1):
         heard = functools.partial(pl.semaphore_wait, ready.at[(1 + dy) // 2], len(partners[dy]))
         if partners[dy]:
             pl.when(greets[dy])(heard)
-    first = [
-        message(3 * q + 3 + side, {"gz": dz, "gy": 2 * side - 1}) for q, dz in enumerate(steps_z)
-    ]
+    first = on_side(ahead, side)
     held = jnp.where(near == 1, 1, 0)
     lax.fori_loop(0, held, bin_own, 0)
     for copy in first:
         copy.start()
-    finish([c for c in bound if c not in across])
-    rest = [message(side, {"gy": 2 * side - 1})]
-    for q, dz in enumerate(steps_z):
-        rest.append(message(3 * q + 4 - side, {"gz": dz, "gy": 1 - 2 * side}))
-    rest.append(message(1 - side, {"gy": 1 - 2 * side}))
-    for q, dz in enumerate(steps_z):
-        rest.append(message(3 * q + 2, {"gz": dz}))
+    finish([c + s for c, _ in behind for s in (0, 1)] + [c + 1 - side for c, _ in ahead] + [c for c, _ in straight])
+    rest = on_side(behind, side)
     for copy in rest:
         copy.start()
+    later = held + 2
+    lax.fori_loop(held, later, bin_own, 0)
+    direct = on_side(ahead, 1 - side) + on_side(behind, 1 - side)
+    direct += [message(c, moves) for c, moves in straight]
+    for copy in direct:
+        copy.start()
+    rest += direct
     copies = first + rest
 
     for side in range(2):
@@ -413,15 +444,17 @@
             pairs.append(masked(prepared(*unpacked(side, i)), got_kind(offsets_x, side, i), (0,)))
         acc_kept[...] += product(pairs)
 
-    lax.fori_loop(held, blocks // GROUP, bin_own, 0)
+    lax.fori_loop(later, blocks // GROUP, bin_own, 0)
 
     total = jnp.concatenate(packed(acc_kept[...]), axis=0)
-    for copy in copies_x + copies_meta + copies:
+    remote(sent_x, got_x, send_x_sem, recv_x_sem.at[0], moves_x[0]).wait_send()
+    for copy in copies_meta:
         copy.wait_send()
-    for c in (3, 6, 1, 2, 4, 5, 7, 8):
-        if c in bound:
-            message(c - 1, classes[c]).wait_recv()
-            total = total + got[c - 1]
+    everything = remote(sent, got, send_sem, recv_sem, classes[1])
+    everything.wait_send()
+    everything.wait_recv()
+    for c in bound:
+        total = total + got[c - 1]
     for h in range(halves):
         here = pl.ds(h * HALF, HALF)
         out_ref[:whole, here] = total[h * whole : (h + 1) * whole]
@@ -453,7 +486,8 @@
             in_specs=[any_space] * 6,
             out_specs=pl.BlockSpec(memory_space=pltpu.VMEM),
             scratch_shapes=[
-                pltpu.VMEM((field_count, particles), f32),
+                pltpu.VMEM((field_count // 8 * 8, particles), f32),
+                pltpu.VMEM((field_count % 8, particles), f32),
                 pltpu.VMEM((blocks, LANES), f32),
                 pltpu.VMEM((blocks, LANES), jnp.int32),
                 pltpu.VMEM((blocks, LANES), jnp.int32),
@@ -472,13 +506,13 @@
                 pltpu.SMEM(block_counts.shape, jnp.int32),
                 pltpu.SMEM(block_lists.shape, jnp.int32),
                 pltpu.VMEM(block_lists.shape, jnp.int32),
-                pltpu.SemaphoreType.DMA((7,)),
-                pltpu.SemaphoreType.DMA((2,)),
+                pltpu.SemaphoreType.DMA((8,)),
+                pltpu.SemaphoreType.DMA,
                 pltpu.SemaphoreType.DMA((2,)),
                 pltpu.SemaphoreType.DMA((len(steps_z),)),
                 pltpu.SemaphoreType.DMA((len(steps_z),)),
-                pltpu.SemaphoreType.DMA((sends,)),
-                pltpu.SemaphoreType.DMA((sends,)),
+                pltpu.SemaphoreType.DMA,
+                pltpu.SemaphoreType.DMA,
                 pltpu.SemaphoreType.REGULAR((2,)),
             ],
             compiler_params=pltpu.CompilerParams(collective_id=0, has_side_effects=True),

time: 13.8 us -> 13.5 us (0.978)
  Pallas kernels: 12.9 us -> 12.7 us
    pallas_call x1, Pallas kernels: 12.9 us -> 12.7 us  [per_device(): pl.pallas_call(functools.partial(migrate_kernel, sizes), out_shape=pltpu....]
where the time goes in v5:
time: 13.5 us; the launch traced here: 13.3 us
  Pallas kernels  12.7 us (94%)
  local copies, waits for them, and re-layouts  0.62 us (5%)
    pallas_call x1, Pallas kernels, per_device(): pl.pallas_call(functools.partial(migrate_kernel, sizes), out_shape=pltpu....  12.7 us
    unnamed x1, local copies, waits for them, and re-layouts  0.62 us

profile of v5, /device:TPU:0, one launch (start us, length us, event | category | flops | bytes accessed | tf_op | source)
XLA Modules:
  0.0 13.3 jit_solution(18360551201576809826)
XLA Ops:
  0.0 12.7 %shard_map.64 = f32[20,512]{1,0:T(8,128)S(1)} custom-call(s32[1,6]{1,0:T(1,128)} %counts_hbm.1, s32[1,48]{1,0:T(1,128)} %lists_hbm.1, f32[20,8192]{1,0:T(8,128)} %fields_hbm.1, f32[64,128]{1,0:T(8,128)} %bitcast.3, s32[64,128]{1,0:T(8,128)} %bitcast.4, s32[64,128]{1,0:T(8,128)} %bitcast.5), custom_call_target="tpu_custom_call" | custom-call | tf_op jit(solution)/shard_map/pallas_call | solution.py:483
  12.7 0.6 %copy.8 = f32[20,512]{1,0:T(8,128)} copy(f32[20,512]{1,0:T(8,128)S(1)} %shard_map.64) | data formatting | bytes 81920

commit v6 on v5

--- a/solution.py
+++ b/solution.py
@@ -106,6 +106,8 @@
     for load in loads:
         load.start()
 
+    near = lax.rem(me["gx"], 2)
+    far = 1 - near
     moves_x = ({"gx": -1}, {"gx": 1})
     partners = {0: [], -1: [], 1: []}
     seen = set()
@@ -189,9 +191,13 @@
         part = pl.ds(first, count)
         return [
             remote(
-                sent_x.at[s, part], got_x.at[s, part], send_x_sem, recv_x_sem.at[s], moves_x[s]
+                sent_x.at[s, part],
+                got_x.at[s, part],
+                send_x_sem,
+                recv_x_sem.at[s],
+                {"gx": 2 * s - 1},
             )
-            for s in range(2)
+            for s in (near, far)
         ]
 
     body_rows = CAP_X * whole
@@ -339,8 +345,6 @@
 
     bound = tuple(range(1, len(classes)))
     y_classes, z_classes = bound[:2], bound[2:]
-    near = lax.rem(me["gx"], 2)
-    far = 1 - near
 
     def got_kind(ref, side, i):
         base = (1 - side) * CAP_X

time: 13.5 us -> 13.5 us (level)
  no operation moved by 1% of the time
where the time goes in v6:
time: 13.5 us; the launch traced here: 13.3 us
  Pallas kernels  12.7 us (94%)
  local copies, waits for them, and re-layouts  0.62 us (5%)
    pallas_call x1, Pallas kernels, per_device(): pl.pallas_call(functools.partial(migrate_kernel, sizes), out_shape=pltpu....  12.7 us
    unnamed x1, local copies, waits for them, and re-layouts  0.62 us

profile of v6, /device:TPU:0, one launch (start us, length us, event | category | flops | bytes accessed | tf_op | source)
XLA Modules:
  0.0 13.3 jit_solution(15256037836238115949)
XLA Ops:
  0.0 12.7 %shard_map.64 = f32[20,512]{1,0:T(8,128)S(1)} custom-call(s32[1,6]{1,0:T(1,128)} %counts_hbm.1, s32[1,48]{1,0:T(1,128)} %lists_hbm.1, f32[20,8192]{1,0:T(8,128)} %fields_hbm.1, f32[64,128]{1,0:T(8,128)} %bitcast.3, s32[64,128]{1,0:T(8,128)} %bitcast.4, s32[64,128]{1,0:T(8,128)} %bitcast.5), custom_call_target="tpu_custom_call" | custom-call | tf_op jit(solution)/shard_map/pallas_call | solution.py:487
  12.7 0.6 %copy.8 = f32[20,512]{1,0:T(8,128)} copy(f32[20,512]{1,0:T(8,128)S(1)} %shard_map.64) | data formatting | bytes 81920
